TPU v7x, 32 devices: a whole 2x2x4 slice. The times are simulated.
32 devices in a mesh: batch: 4 (over z), row: 4 (over x, core), col: 2 (over y).
Axes of the slice: x: 2, y: 2, z: 4, core: 2. Of those that a mesh axis runs over, the one named last changes fastest.
Arguments:
- flows: float32 [32768, 8192], P(('batch', 'row'), 'col'), parts along dimension 0, may hold values from 0 to 21, as said below
- tile_mask: int32 [256, 64], P(('batch', 'row'), 'col'), parts along dimension 0, may hold values from 0 to 1, as said below
- row_target: int32 [32768], P(('batch', 'row')), parts along dimension 0, may hold values from 1638400 to 8191999
- col_target: int32 [32768], P(('batch', 'col')), parts along dimension 0, may hold values from 1638400 to 8191999
Outputs:
- row_history: float32 [12, 8192], P('batch', 'row'), parts along dimension 0
- col_history: float32 [12, 8192], P('batch', 'col'), parts along dimension 0
There are 4 independent parts, one for each index of `batch`. A program takes and returns all parts, laid end to end along the dimension named above; each array names one. Nothing has to cross between parts.
Inputs may be any that keep to these rules, and one draw needn't show every extreme that they name: `tile_mask`: every diagonal tile is 1. `flows`: every entry is positive.
All inputs are finite; a program needn't handle non-finite values.
Results may differ from a plain program's by a relative error of at most 0.0001.
Values sent between devices are 32-bit elements; how exact they have to be, the bound alone decides.
A program may use at most 192 MiB of HBM per device.

v0:
```python
import jax
import jax.numpy as jnp
from jax import lax
from jax.sharding import PartitionSpec as P

ITERS = 3


def block_sweeps(active, row_goal, col_goal):
    row_count, col_count = active.shape
    row_hist = jnp.zeros((ITERS, row_count), jnp.float32)
    col_hist = jnp.zeros((ITERS, col_count), jnp.float32)
    col_scale = jnp.ones((col_count,), jnp.float32)

    def advance(sweep_index, carry):
        col_scale, row_hist, col_hist = carry
        row_part = jnp.sum(active * col_scale[None, :], axis=1)
        row_total = lax.psum(row_part, "col")
        row_scale = row_goal / row_total
        col_part = jnp.sum(active * row_scale[:, None], axis=0)
        col_total = lax.psum(col_part, "row")
        col_scale = col_goal / col_total
        row_hist = lax.dynamic_update_slice_in_dim(row_hist, row_scale[None, :], sweep_index, 0)
        col_hist = lax.dynamic_update_slice_in_dim(col_hist, col_scale[None, :], sweep_index, 0)
        return (col_scale, row_hist, col_hist)

    col_scale, row_hist, col_hist = lax.fori_loop(
        0, ITERS, advance, (col_scale, row_hist, col_hist)
    )
    return (row_hist, col_hist)


def shards(flows, tile_mask, row_target, col_target):
    row_count, col_count = flows.shape
    tile_side = row_count // tile_mask.shape[0]
    expand = tile_mask.astype(jnp.float32)[:, None, :, None]
    active = (
        flows.reshape(row_count // tile_side, tile_side, col_count // tile_side, tile_side) * expand
    ).reshape(row_count, col_count)
    row_goal = row_target.astype(jnp.float32) * 0.001
    col_goal = col_target.astype(jnp.float32) * 0.001
    row_hist, col_hist = block_sweeps(active, row_goal, col_goal)
    return (row_hist, col_hist)


def solution(mesh):
    return jax.shard_map(
        shards,
        mesh=mesh,
        in_specs=(
            P(("batch", "row"), "col"),
            P(("batch", "row"), "col"),
            P(("batch", "row")),
            P(("batch", "col")),
        ),
        out_specs=(P("batch", "row"), P("batch", "col")),
        check_vma=False,
    )
```

profile of v0, /device:TPU:0, one launch (start us, length us, event | category | flops | bytes accessed | tf_op | source)
XLA Modules:
  0.0 185.6 jit_solution(14115084264689669346)
XLA Ops:
  0.6 0.7 convert_element_type.9
  1.3 11.2 %mul.63 = f32[16,128,32,128]{3,2,1,0:T(8,128)} broadcast(f32[16,32]{1,0:T(8,128)S(1)} %convert_element_type.9), dimensions={0,2} | broadcast | bytes 33556480 | tf_op jit(solution)/shard_map/mul | solution.py:38
  12.6 0.0 copy-start
  12.6 0.0 copy-start.1
  12.6 42.4 %bitcast_multiply_fusion = f32[2048,4096]{1,0:T(8,128)} fusion(f32[2048,4096]{1,0:T(8,128)} %param.6, f32[256,8,32,128]{3,2,1,0:T(8,128)} %bitcast.10), kind=kLoop, calls=%fused_computation.3 | loop fusion | flops 8388608 | bytes 100663296 | tf_op jit(solution)/shard_map/mul | solution.py:38
  55.0 0.0 copy-done
  55.0 0.0 copy-done.1
  55.0 130.6 %while.18 = (s32[]{:T(128)}, f32[4096]{0:T(1024)S(1)}, f32[3,2048]{1,0:T(4,128)}, f32[3,4096]{1,0:T(4,128)}, f32[2048,4096]{1,0:T(8,128)}, /*index=5*/f32[2048]{0:T(1024)S(1)}, f32[4096]{0:T(1024)S(1)}, s32[]{:T(128)}, s32[]{:T(128)}) while((s32[]{:T(128)}, f32[4096]{0:T(1024)S(1)}, f32[3,2048]{1,0:T(4,128)}, f32[3,4096]{1,0:T(4,128)}, ...), condition=%wide.region_5.0_spmd.clone, body=%wide.region_0.0_spmd.clone.sunk | while | flops 33564672 | bytes 67362928 | solution.py:27
  55.1 12.3 %multiply_reduce_fusion.4 = f32[2048]{0:T(1024)S(1)} fusion(f32[2048,4096]{1,0:T(8,128)} %get-tuple-element.232, f32[4096]{0:T(1024)S(1)} %broadcast_select_fusion.2), kind=kLoop, calls=%fused_computation.1.clone.1 | loop fusion | flops 16775168 | bytes 33579008 | tf_op jit(solution)/shard_map/while/body/eval_jaxpr/reduce_sum | solution.py:17
  67.3 6.0 %psum.26 = f32[2048]{0:T(1024)S(1)} all-reduce(f32[2048]{0:T(1024)S(1)} %multiply_reduce_fusion.4), channel_id=1, replica_groups=mesh['batch'=4,'row'=4,'col'=2] {'col'}, use_global_device_ids=true, to_apply=%region_2.0 | all-reduce | flops 2048 | bytes 16384 | tf_op jit(solution)/shard_map/while/body/eval_jaxpr/psum | solution.py:18
  73.3 12.8 %multiply_reduce_fusion.5 = f32[4096]{0:T(1024)S(1)} fusion(f32[2048,4096]{1,0:T(8,128)} %get-tuple-element.232, f32[2048]{0:T(1024)S(1)} %div.18), kind=kLoop, calls=%fused_computation.clone.1 | loop fusion | flops 16773120 | bytes 33579008 | tf_op jit(solution)/shard_map/while/body/eval_jaxpr/reduce_sum | solution.py:20
  86.1 10.3 %psum.27 = f32[4096]{0:T(1024)S(1)} all-reduce(f32[4096]{0:T(1024)S(1)} %multiply_reduce_fusion.5), channel_id=1, replica_groups=mesh['batch'=4,'row'=4,'col'=2] {'row'}, use_global_device_ids=true, to_apply=%region_4.0 | all-reduce | flops 4096 | bytes 32768 | tf_op jit(solution)/shard_map/while/body/eval_jaxpr/psum | solution.py:21
  96.4 1.5 dynamic_update_slice.19
  97.9 1.4 dynamic_update_slice.18
  99.3 12.2 %multiply_reduce_fusion.4 = f32[2048]{0:T(1024)S(1)} fusion(f32[2048,4096]{1,0:T(8,128)} %get-tuple-element.232, f32[4096]{0:T(1024)S(1)} %broadcast_select_fusion.2), kind=kLoop, calls=%fused_computation.1.clone.1 | loop fusion | flops 16775168 | bytes 33579008 | tf_op jit(solution)/shard_map/while/body/eval_jaxpr/reduce_sum | solution.py:17
  111.6 5.0 %psum.26 = f32[2048]{0:T(1024)S(1)} all-reduce(f32[2048]{0:T(1024)S(1)} %multiply_reduce_fusion.4), channel_id=1, replica_groups=mesh['batch'=4,'row'=4,'col'=2] {'col'}, use_global_device_ids=true, to_apply=%region_2.0 | all-reduce | flops 2048 | bytes 16384 | tf_op jit(solution)/shard_map/while/body/eval_jaxpr/psum | solution.py:18
  116.6 12.8 %multiply_reduce_fusion.5 = f32[4096]{0:T(1024)S(1)} fusion(f32[2048,4096]{1,0:T(8,128)} %get-tuple-element.232, f32[2048]{0:T(1024)S(1)} %div.18), kind=kLoop, calls=%fused_computation.clone.1 | loop fusion | flops 16773120 | bytes 33579008 | tf_op jit(solution)/shard_map/while/body/eval_jaxpr/reduce_sum | solution.py:20
  129.4 10.1 %psum.27 = f32[4096]{0:T(1024)S(1)} all-reduce(f32[4096]{0:T(1024)S(1)} %multiply_reduce_fusion.5), channel_id=1, replica_groups=mesh['batch'=4,'row'=4,'col'=2] {'row'}, use_global_device_ids=true, to_apply=%region_4.0 | all-reduce | flops 4096 | bytes 32768 | tf_op jit(solution)/shard_map/while/body/eval_jaxpr/psum | solution.py:21
  139.5 1.5 dynamic_update_slice.19
  141.1 1.4 dynamic_update_slice.18
  142.5 12.2 %multiply_reduce_fusion.4 = f32[2048]{0:T(1024)S(1)} fusion(f32[2048,4096]{1,0:T(8,128)} %get-tuple-element.232, f32[4096]{0:T(1024)S(1)} %broadcast_select_fusion.2), kind=kLoop, calls=%fused_computation.1.clone.1 | loop fusion | flops 16775168 | bytes 33579008 | tf_op jit(solution)/shard_map/while/body/eval_jaxpr/reduce_sum | solution.py:17
  154.7 5.0 %psum.26 = f32[2048]{0:T(1024)S(1)} all-reduce(f32[2048]{0:T(1024)S(1)} %multiply_reduce_fusion.4), channel_id=1, replica_groups=mesh['batch'=4,'row'=4,'col'=2] {'col'}, use_global_device_ids=true, to_apply=%region_2.0 | all-reduce | flops 2048 | bytes 16384 | tf_op jit(solution)/shard_map/while/body/eval_jaxpr/psum | solution.py:18
  159.7 12.8 %multiply_reduce_fusion.5 = f32[4096]{0:T(1024)S(1)} fusion(f32[2048,4096]{1,0:T(8,128)} %get-tuple-element.232, f32[2048]{0:T(1024)S(1)} %div.18), kind=kLoop, calls=%fused_computation.clone.1 | loop fusion | flops 16773120 | bytes 33579008 | tf_op jit(solution)/shard_map/while/body/eval_jaxpr/reduce_sum | solution.py:20
  172.5 10.1 %psum.27 = f32[4096]{0:T(1024)S(1)} all-reduce(f32[4096]{0:T(1024)S(1)} %multiply_reduce_fusion.5), channel_id=1, replica_groups=mesh['batch'=4,'row'=4,'col'=2] {'row'}, use_global_device_ids=true, to_apply=%region_4.0 | all-reduce | flops 4096 | bytes 32768 | tf_op jit(solution)/shard_map/while/body/eval_jaxpr/psum | solution.py:21
  182.7 1.5 dynamic_update_slice.19
  184.2 1.4 dynamic_update_slice.18
  (14 shorter events, 0.1 us)
Async XLA Ops:
  12.6 42.4 %copy-start = (s32[4096]{0:T(1024)S(1)}, s32[4096]{0:T(1024)}, u32[]{:S(2)}) copy-start(s32[4096]{0:T(1024)} %param.9) | copy-start | bytes 49156
  12.6 42.5 %copy-start.1 = (s32[2048]{0:T(1024)S(1)}, s32[2048]{0:T(1024)}, u32[]{:S(2)}) copy-start(s32[2048]{0:T(1024)} %param.8) | copy-start | bytes 24580
where the time goes:
time: 187 us; the launch traced here: 186 us
  other arithmetic  118 us (63%)
  blocking collectives  46.5 us (25%)
  local copies, waits for them, and re-layouts  20.1 us (11%)
    mul x1, other arithmetic, shards(): flows.reshape(row_count // tile_side, tile_side, col_count // tile_side,...  42.4 us
    reduce_sum x3, other arithmetic, advance(): col_part = jnp.sum(active * row_scale[:, None], axis=0)  38.4 us
    reduce_sum x3, other arithmetic, advance(): row_part = jnp.sum(active * col_scale[None, :], axis=1)  36.8 us
    psum x3, blocking collectives, advance(): col_total = lax.psum(col_part, 'row')  30.5 us
    psum x3, blocking collectives, advance(): row_total = lax.psum(row_part, 'col')  16 us
    mul x1, local copies, waits for them, and re-layouts, shards(): flows.reshape(row_count // tile_side, tile_side, col_count // tile_side,...  11.2 us
    dynamic_update_slice x3, local copies, waits for them, and re-layouts, advance(): lax.dynamic_update_slice_in_dim(col_hist, col_scale[None, :], sweep_index...  4.64 us
    dynamic_update_slice x3, local copies, waits for them, and re-layouts, advance(): lax.dynamic_update_slice_in_dim(row_hist, row_scale[None, :], sweep_index...  4.23 us

commit v1 on v0

--- a/solution.py
+++ b/solution.py
@@ -18,7 +18,8 @@
         row_total = lax.psum(row_part, "col")
         row_scale = row_goal / row_total
         col_part = jnp.sum(active * row_scale[:, None], axis=0)
-        col_total = lax.psum(col_part, "row")
+        parts = lax.all_gather(col_part, "row", axis=0, tiled=False)
+        col_total = parts.sum(axis=0)
         col_scale = col_goal / col_total
         row_hist = lax.dynamic_update_slice_in_dim(row_hist, row_scale[None, :], sweep_index, 0)
         col_hist = lax.dynamic_update_slice_in_dim(col_hist, col_scale[None, :], sweep_index, 0)

time: 187 us -> 172 us (0.920)
  blocking collectives: 46.5 us -> 31.7 us
    psum x3 -> x0, blocking collectives: 30.5 us -> none  [advance(): col_total = lax.psum(col_part, 'row')]
    all_gather x0 -> x3, blocking collectives: none -> 15.7 us  [advance(): parts = lax.all_gather(col_part, 'row', axis=0, tiled=False)]
where the time goes in v1:
time: 172 us; the launch traced here: 171 us
  other arithmetic  118 us (69%)
  blocking collectives  31.7 us (18%)
  local copies, waits for them, and re-layouts  20.2 us (12%)
    mul x1, other arithmetic, shards(): flows.reshape(row_count // tile_side, tile_side, col_count // tile_side,...  42.4 us
    reduce_sum x3, other arithmetic, advance(): col_part = jnp.sum(active * row_scale[:, None], axis=0)  38.3 us
    reduce_sum x3, other arithmetic, advance(): row_part = jnp.sum(active * col_scale[None, :], axis=1)  36.8 us
    psum x3, blocking collectives, advance(): row_total = lax.psum(row_part, 'col')  16 us
    all_gather x3, blocking collectives, advance(): parts = lax.all_gather(col_part, 'row', axis=0, tiled=False)  15.7 us
    mul x1, local copies, waits for them, and re-layouts, shards(): flows.reshape(row_count // tile_side, tile_side, col_count // tile_side,...  11.2 us
    dynamic_update_slice x3, local copies, waits for them, and re-layouts, advance(): lax.dynamic_update_slice_in_dim(col_hist, col_scale[None, :], sweep_index...  4.65 us
    dynamic_update_slice x3, local copies, waits for them, and re-layouts, advance(): lax.dynamic_update_slice_in_dim(row_hist, row_scale[None, :], sweep_index...  4.23 us

profile of v1, /device:TPU:0, one launch (start us, length us, event | category | flops | bytes accessed | tf_op | source)
XLA Modules:
  0.0 171.1 jit_solution(4734910486168793281)
XLA Ops:
  0.6 0.7 convert_element_type.9
  1.3 11.2 %mul.63 = f32[16,128,32,128]{3,2,1,0:T(8,128)} broadcast(f32[16,32]{1,0:T(8,128)S(1)} %convert_element_type.9), dimensions={0,2} | broadcast | bytes 33556480 | tf_op jit(solution)/shard_map/mul | solution.py:39
  12.6 0.0 copy-start
  12.6 0.0 copy-start.1
  12.6 42.4 %bitcast_multiply_fusion = f32[2048,4096]{1,0:T(8,128)} fusion(f32[2048,4096]{1,0:T(8,128)} %param.6, f32[256,8,32,128]{3,2,1,0:T(8,128)} %bitcast.10), kind=kLoop, calls=%fused_computation.3 | loop fusion | flops 8388608 | bytes 100663296 | tf_op jit(solution)/shard_map/mul | solution.py:39
  55.0 0.0 copy-done
  55.0 0.0 copy-done.1
  55.0 116.1 %while.18 = (s32[]{:T(128)}, f32[4096]{0:T(1024)S(1)}, f32[3,2048]{1,0:T(4,128)}, f32[3,4096]{1,0:T(4,128)}, f32[2048,4096]{1,0:T(8,128)}, /*index=5*/f32[2048]{...) while((s32[]{:T(128)}, f32[4096]{0:T(1024)S(1)}, f32[3,2048]{1,0:T(4,128)}, ...), condition=%wide.region_5.0_spmd.clone, body=%wide.region_0.0_spmd.clone.sunk | while | flops 33572864 | bytes 67625080 | solution.py:28
  55.1 12.3 %multiply_reduce_fusion.4 = f32[2048]{0:T(1024)S(1)} fusion(f32[2048,4096]{1,0:T(8,128)} %get-tuple-element.234, f32[4096]{0:T(1024)S(1)} %broadcast_select_fusion.2), kind=kLoop, calls=%fused_computation.1.clone.1 | loop fusion | flops 16775168 | bytes 33579008 | tf_op jit(solution)/shard_map/while/body/eval_jaxpr/reduce_sum | solution.py:17
  67.3 6.0 %psum.13 = f32[2048]{0:T(1024)S(1)} all-reduce(f32[2048]{0:T(1024)S(1)} %multiply_reduce_fusion.4), channel_id=1, replica_groups=mesh['batch'=4,'row'=4,'col'=2] {'col'}, use_global_device_ids=true, to_apply=%region_2.0 | all-reduce | flops 2048 | bytes 16384 | tf_op jit(solution)/shard_map/while/body/eval_jaxpr/psum | solution.py:18
  73.3 12.8 %multiply_reduce_fusion.5 = f32[4096]{0:T(1024)S(1)} fusion(f32[2048,4096]{1,0:T(8,128)} %get-tuple-element.234, f32[2048]{0:T(1024)S(1)} %div.31), kind=kLoop, calls=%fused_computation.clone.1 | loop fusion | flops 16773120 | bytes 33579008 | tf_op jit(solution)/shard_map/while/body/eval_jaxpr/reduce_sum | solution.py:20
  86.1 5.2 %all-gather.3 = f32[16384]{0:T(1024)S(1)} all-gather(f32[4096]{0:T(1024)S(1)} %multiply_reduce_fusion.5), channel_id=2, replica_groups=mesh['batch'=4,'row'=4,'col'=2] {'row'}, dimensions={0}, use_global_device_ids=true | all-gather | bytes 81920 | tf_op jit(solution)/shard_map/while/body/eval_jaxpr/all_gather | solution.py:21
  91.4 1.5 dynamic_update_slice.19
  93.0 1.4 dynamic_update_slice.18
  94.4 12.2 %multiply_reduce_fusion.4 = f32[2048]{0:T(1024)S(1)} fusion(f32[2048,4096]{1,0:T(8,128)} %get-tuple-element.234, f32[4096]{0:T(1024)S(1)} %broadcast_select_fusion.2), kind=kLoop, calls=%fused_computation.1.clone.1 | loop fusion | flops 16775168 | bytes 33579008 | tf_op jit(solution)/shard_map/while/body/eval_jaxpr/reduce_sum | solution.py:17
  106.6 5.0 %psum.13 = f32[2048]{0:T(1024)S(1)} all-reduce(f32[2048]{0:T(1024)S(1)} %multiply_reduce_fusion.4), channel_id=1, replica_groups=mesh['batch'=4,'row'=4,'col'=2] {'col'}, use_global_device_ids=true, to_apply=%region_2.0 | all-reduce | flops 2048 | bytes 16384 | tf_op jit(solution)/shard_map/while/body/eval_jaxpr/psum | solution.py:18
  111.7 12.8 %multiply_reduce_fusion.5 = f32[4096]{0:T(1024)S(1)} fusion(f32[2048,4096]{1,0:T(8,128)} %get-tuple-element.234, f32[2048]{0:T(1024)S(1)} %div.31), kind=kLoop, calls=%fused_computation.clone.1 | loop fusion | flops 16773120 | bytes 33579008 | tf_op jit(solution)/shard_map/while/body/eval_jaxpr/reduce_sum | solution.py:20
  124.4 5.2 %all-gather.3 = f32[16384]{0:T(1024)S(1)} all-gather(f32[4096]{0:T(1024)S(1)} %multiply_reduce_fusion.5), channel_id=2, replica_groups=mesh['batch'=4,'row'=4,'col'=2] {'row'}, dimensions={0}, use_global_device_ids=true | all-gather | bytes 81920 | tf_op jit(solution)/shard_map/while/body/eval_jaxpr/all_gather | solution.py:21
  129.8 1.5 dynamic_update_slice.19
  131.3 1.4 dynamic_update_slice.18
  132.7 12.2 %multiply_reduce_fusion.4 = f32[2048]{0:T(1024)S(1)} fusion(f32[2048,4096]{1,0:T(8,128)} %get-tuple-element.234, f32[4096]{0:T(1024)S(1)} %broadcast_select_fusion.2), kind=kLoop, calls=%fused_computation.1.clone.1 | loop fusion | flops 16775168 | bytes 33579008 | tf_op jit(solution)/shard_map/while/body/eval_jaxpr/reduce_sum | solution.py:17
  145.0 5.0 %psum.13 = f32[2048]{0:T(1024)S(1)} all-reduce(f32[2048]{0:T(1024)S(1)} %multiply_reduce_fusion.4), channel_id=1, replica_groups=mesh['batch'=4,'row'=4,'col'=2] {'col'}, use_global_device_ids=true, to_apply=%region_2.0 | all-reduce | flops 2048 | bytes 16384 | tf_op jit(solution)/shard_map/while/body/eval_jaxpr/psum | solution.py:18
  150.0 12.8 %multiply_reduce_fusion.5 = f32[4096]{0:T(1024)S(1)} fusion(f32[2048,4096]{1,0:T(8,128)} %get-tuple-element.234, f32[2048]{0:T(1024)S(1)} %div.31), kind=kLoop, calls=%fused_computation.clone.1 | loop fusion | flops 16773120 | bytes 33579008 | tf_op jit(solution)/shard_map/while/body/eval_jaxpr/reduce_sum | solution.py:20
  162.8 5.2 %all-gather.3 = f32[16384]{0:T(1024)S(1)} all-gather(f32[4096]{0:T(1024)S(1)} %multiply_reduce_fusion.5), channel_id=2, replica_groups=mesh['batch'=4,'row'=4,'col'=2] {'row'}, dimensions={0}, use_global_device_ids=true | all-gather | bytes 81920 | tf_op jit(solution)/shard_map/while/body/eval_jaxpr/all_gather | solution.py:21
  168.1 1.5 dynamic_update_slice.19
  169.7 1.4 dynamic_update_slice.18
  (20 shorter events, 0.3 us)
Async XLA Ops:
  12.6 42.4 %copy-start = (s32[4096]{0:T(1024)S(1)}, s32[4096]{0:T(1024)}, u32[]{:S(2)}) copy-start(s32[4096]{0:T(1024)} %param.9) | copy-start | bytes 49156
  12.6 42.5 %copy-start.1 = (s32[2048]{0:T(1024)S(1)}, s32[2048]{0:T(1024)}, u32[]{:S(2)}) copy-start(s32[2048]{0:T(1024)} %param.8) | copy-start | bytes 24580
